TPU v7x, 32 devices: a whole 2x2x4 slice. The times are simulated.
32 devices in a mesh: lat: 16 (over z, y, x), batch: 2 (over core).
Axes of the slice: x: 2, y: 2, z: 4, core: 2. Of those that a mesh axis runs over, the one named last changes fastest.
Arguments:
- fields: bfloat16 [2, 192, 384, 384], P('batch', 'lat'), may hold values from -6 to 6
- cotangent: bfloat16 [2, 192, 384, 384], P('batch', 'lat'), may hold values from -6 to 6
- weights: bfloat16 [128, 2, 384, 384], P('lat'), may hold values from -0.21875 to 0.21875
- degree_of: int32 [128], replicated, may hold values from 0 to 127, each once
Outputs:
- grad_fields: bfloat16 [2, 192, 384, 384], P('batch', 'lat')
- grad_weights: bfloat16 [128, 2, 384, 384], P('lat')
Inputs may be any that keep to these rules, and one draw needn't show every extreme that they name: `degree_of`: each degree 0 to 127 is held by exactly one slot.
All inputs are finite; a program needn't handle non-finite values.
Results may differ from a plain program's by a relative error of at most 0.018.
Values may be sent and summed in bfloat16 or wider, within the bound.
A program may use at most 64 MiB of HBM per device.

v0:
```python
import jax
import jax.numpy as jnp
from jax import lax
from jax.sharding import PartitionSpec as P

LATS = 192
LONS = 384
ORDERS = 128
DEGREES = 128
CHANNELS = 384


def legendre_table(order_ids, lat_count, degree_count):
    colatitude = jnp.pi * (jnp.arange(lat_count, dtype=jnp.float32) + 0.5) / lat_count
    cosine = jnp.cos(colatitude)[None, :]
    log_sine = jnp.log(jnp.sin(colatitude))[None, :]
    order_col = order_ids[:, None]
    order_real = order_col.astype(jnp.float32)
    steps_up = jnp.arange(1, degree_count + 1, dtype=jnp.float32)[None, :]
    factor = jnp.where(
        steps_up <= order_real, 0.5 * jnp.log((2.0 * steps_up + 1.0) / (2.0 * steps_up)), 0.0
    )
    log_start = 0.5 * jnp.log(1.0 / (4.0 * jnp.pi)) + jnp.sum(factor, axis=1, keepdims=True)
    diagonal = jnp.exp(log_start + order_real * log_sine)
    squared = order_real * order_real

    def advance(carry, degree):
        previous, older = carry
        degree_real = degree.astype(jnp.float32)
        lead = jnp.sqrt(
            jnp.maximum(4.0 * degree_real * degree_real - 1.0, 0.0)
            / jnp.maximum(degree_real * degree_real - squared, 1.0)
        )
        lower = degree_real - 1.0
        back = jnp.sqrt(
            jnp.maximum(lower * lower - squared, 0.0) / jnp.maximum(4.0 * lower * lower - 1.0, 1.0)
        )
        general = lead * (cosine * previous - back * older)
        first = jnp.sqrt(2.0 * order_real + 3.0) * cosine * previous
        value = jnp.where(
            degree == order_col,
            diagonal,
            jnp.where(
                degree == order_col + 1, first, jnp.where(degree > order_col + 1, general, 0.0)
            ),
        )
        return ((value, previous), value)

    zeros = jnp.zeros((order_ids.shape[0], lat_count), jnp.float32)
    final_state, table = lax.scan(
        advance, (zeros, zeros), jnp.arange(degree_count, dtype=jnp.int32)
    )
    return jnp.transpose(table, (1, 0, 2))


def spectral_tables(start, ord_dev, degree_of):
    order_ids = start + jnp.arange(ord_dev, dtype=jnp.int32)
    mine = legendre_table(order_ids, LATS, DEGREES)
    selector = (degree_of[:, None] == jnp.arange(DEGREES, dtype=jnp.int32)[None, :]).astype(
        jnp.float32
    )
    chosen = jnp.einsum("mli,jl->mji", mine, selector, precision=lax.Precision.HIGHEST)
    colatitude = jnp.pi * (jnp.arange(LATS, dtype=jnp.float32) + 0.5) / LATS
    quadrature = 2.0 * jnp.pi * jnp.pi / LATS * jnp.sin(colatitude)
    return ((chosen * quadrature[None, None, :]).astype(jnp.bfloat16), chosen.astype(jnp.bfloat16))


def fourier_tables(lon_count, order_count):
    lon_ids = jnp.arange(lon_count, dtype=jnp.int32)[:, None]
    order_ids = jnp.arange(order_count, dtype=jnp.int32)[None, :]
    phase = 2.0 * jnp.pi * (lon_ids * order_ids % lon_count).astype(jnp.float32) / lon_count
    forward = (
        jnp.stack([jnp.cos(phase), -jnp.sin(phase)], axis=2).reshape(lon_count, 2 * order_count)
        / lon_count
    )
    doubled = jnp.where(order_ids == 0, 1.0, 2.0)
    inverse = jnp.stack([doubled * jnp.cos(phase), -doubled * jnp.sin(phase)], axis=2).reshape(
        lon_count, 2 * order_count
    )
    return (forward.astype(jnp.bfloat16), jnp.transpose(inverse).astype(jnp.bfloat16))


def to_orders(values):
    return lax.all_to_all(values, "lat", split_axis=1, concat_axis=0, tiled=True)


def to_degrees(values):
    return lax.all_to_all(values, "lat", split_axis=0, concat_axis=1, tiled=True)


def back_to_orders(values):
    return lax.all_to_all(values, "lat", split_axis=1, concat_axis=0, tiled=True)


def to_bands(values):
    return lax.all_to_all(values, "lat", split_axis=0, concat_axis=1, tiled=True)


def product(spec, left, right):
    return jnp.einsum(spec, left, right, preferred_element_type=jnp.float32)


def apply_filter(coeffs, weights):
    c_real = coeffs[:, :, 0]
    c_imag = coeffs[:, :, 1]
    w_real = weights[:, 0]
    w_imag = weights[:, 1]
    f_real = product("jmsc,jcd->jmsd", c_real, w_real) - product("jmsc,jcd->jmsd", c_imag, w_imag)
    f_imag = product("jmsc,jcd->jmsd", c_real, w_imag) + product("jmsc,jcd->jmsd", c_imag, w_real)
    return jnp.stack([f_real, f_imag], axis=2).astype(jnp.bfloat16)


def adjoint_filter(grads, weights):
    g_real = grads[:, :, 0]
    g_imag = grads[:, :, 1]
    w_real = weights[:, 0]
    w_imag = weights[:, 1]
    a_real = product("jmsd,jcd->jmsc", g_real, w_real) + product("jmsd,jcd->jmsc", g_imag, w_imag)
    a_imag = product("jmsd,jcd->jmsc", g_imag, w_real) - product("jmsd,jcd->jmsc", g_real, w_imag)
    return jnp.stack([a_real, a_imag], axis=2).astype(jnp.bfloat16)


def filter_grad(coeffs, grads):
    c_real = coeffs[:, :, 0]
    c_imag = coeffs[:, :, 1]
    g_real = grads[:, :, 0]
    g_imag = grads[:, :, 1]
    dw_real = product("jmsc,jmsd->jcd", c_real, g_real) + product("jmsc,jmsd->jcd", c_imag, g_imag)
    dw_imag = product("jmsc,jmsd->jcd", c_real, g_imag) - product("jmsc,jmsd->jcd", c_imag, g_real)
    return jnp.stack([dw_real, dw_imag], axis=1)


def local(fields, cotangent, weights, degree_of):
    samples = fields.shape[0]
    band_rows = fields.shape[1]
    ord_dev = ORDERS // lax.axis_size("lat")
    forward, inverse = fourier_tables(LONS, ORDERS)
    qslot, pslot = spectral_tables(lax.axis_index("lat") * ord_dev, ord_dev, degree_of)
    spectra = product("sikc,kf->ifsc", fields, forward).astype(jnp.bfloat16)
    spectra = spectra.reshape(band_rows, ORDERS, 2, samples, CHANNELS)
    gathered = to_orders(spectra)
    coeffs_local = product("mji,imrsc->jmrsc", qslot, gathered).astype(jnp.bfloat16)
    coeffs = to_degrees(coeffs_local)
    filtered = apply_filter(coeffs, weights)
    returned = back_to_orders(filtered)
    synth_local = product("mji,jmrsc->imrsc", pslot, returned).astype(jnp.bfloat16)
    synth = to_bands(synth_local)
    response = product(
        "ifsc,fk->sikc", synth.reshape(band_rows, 2 * ORDERS, samples, CHANNELS), inverse
    )
    activated, pullback = jax.vjp(jax.nn.gelu, response)
    upstream = pullback(cotangent.astype(jnp.float32))[0].astype(jnp.bfloat16)
    grad_synth = product("sikc,fk->ifsc", upstream, inverse).astype(jnp.bfloat16)
    grad_synth = grad_synth.reshape(band_rows, ORDERS, 2, samples, CHANNELS)
    grad_gathered = to_orders(grad_synth)
    grad_local = product("mji,imrsc->jmrsc", pslot, grad_gathered).astype(jnp.bfloat16)
    grad_filtered = to_degrees(grad_local)
    weight_total = lax.psum(filter_grad(coeffs, grad_filtered).astype(jnp.bfloat16), "batch")
    grad_coeffs = adjoint_filter(grad_filtered, weights)
    grad_back = back_to_orders(grad_coeffs)
    grad_local_spec = product("mji,jmrsc->imrsc", qslot, grad_back).astype(jnp.bfloat16)
    grad_bands = to_bands(grad_local_spec)
    delta = product(
        "ifsc,kf->sikc", grad_bands.reshape(band_rows, 2 * ORDERS, samples, CHANNELS), forward
    )
    grad_fields = (cotangent.astype(jnp.float32) + delta).astype(jnp.bfloat16)
    return (grad_fields, weight_total)


def solution(mesh):
    return jax.shard_map(
        local,
        mesh=mesh,
        in_specs=(
            P("batch", "lat", None, None),
            P("batch", "lat", None, None),
            P("lat", None, None, None),
            P(),
        ),
        out_specs=(P("batch", "lat", None, None), P("lat", None, None, None)),
        check_vma=False,
    )
```

profile of v0, /device:TPU:12, one launch (start us, length us, event | category | flops | bytes accessed | tf_op | source)
XLA Modules:
  0.0 810.5 jit_solution(15554122631083850034)
XLA Ops:
  7.2 0.8 fusion.118
  8.0 0.7 fusion.105
  8.7 1.8 copy.176
  10.5 1.7 reshape.493
  12.2 3.7 convert_bitcast_fusion.3
  15.9 4.8 reshape.480
  20.8 3.0 copy.178
  23.8 7.2 all-to-all-start
  31.3 351.8 %while.21 = (s32[]{:T(128)}, f32[8,192]{1,0:T(8,128)S(1)}, f32[8,192]{1,0:T(8,128)S(1)}, f32[128,8,192]{2,1,0:T(8,128)S(1)}, s32[128]{0:T(128)S(1)}, /*index=5*/...) while((s32[]{:T(128)}, f32[8,192]{1,0:T(8,128)S(1)}, ...), condition=%wide.region_2.3_spmd.clone.clone.clone.clone, body=%wide.region_1.2_spmd.clone.clone.clone.clone.sunk | while | flops 18991 | bytes 48339 | solution.py:50
  51.8 0.6 compare_bitcast_fusion.5
  54.6 0.6 compare_bitcast_fusion.5
  57.3 0.6 compare_bitcast_fusion.5
  60.1 0.6 compare_bitcast_fusion.5
  62.8 0.6 compare_bitcast_fusion.5
  65.6 0.6 compare_bitcast_fusion.5
  68.3 0.6 compare_bitcast_fusion.5
  71.1 0.6 compare_bitcast_fusion.5
  73.8 0.6 compare_bitcast_fusion.5
  384.1 2.1 copy.249
  386.6 1.4 fusion.79
  388.0 2.9 copy.183
  390.9 43.5 %all_to_all.126 = bf16[128,8,2,1,384]{4,2,1,3,0:T(2,128)(2,1)S(1)} all-to-all(bf16[128,8,2,1,384]{4,2,1,3,0:T(2,128)(2,1)} %copy.183), channel_id=1, replica_groups=mesh['lat'=16,'batch'=2] {'lat'}, dimensions={0} | all-to-all | bytes 3145728 | tf_op jit(solution)/shard_map/all_to_all | solution.py:88
  435.1 0.7 fusion.40
  435.7 0.7 fusion.38
  436.4 0.7 fusion.90
  437.1 0.7 fusion.93
  438.0 0.9 copy.188
  439.0 40.7 %all_to_all.127 = bf16[8,128,2,1,384]{4,0,3,2,1:T(8,128)(2,1)S(1)} all-to-all(bf16[8,128,2,1,384]{4,0,3,2,1:T(8,128)(2,1)S(1)} %copy.188), channel_id=1, replica_groups=mesh['lat'=16,'batch'=2] {'lat'}, dimensions={1} | all-to-all | bytes 3145728 | tf_op jit(solution)/shard_map/all_to_all | solution.py:92
  479.7 0.8 convert_bitcast_fusion.2
  480.4 3.8 copy.190
  484.3 5.8 all-to-all-start.3
  490.1 0.8 multiply_convert_fusion.1
  491.4 51.3 %all-to-all-done.3 = bf16[192,8,2,1,384]{4,2,1,3,0:T(2,128)(2,1)} async-done(((bf16[192,8,2,1,384]{4,2,1,3,0:T(2,128)(2,1)}), bf16[192,8,2,1,384]{4,2,1,3,0:T(2,128)(2,1)}, u32[]{:S(2)}, u32[]{:S(2)}) %all-to-all-start.3) | async-done | bytes 2359328 | tf_op jit(solution)/shard_map/all_to_all | solution.py:96
  542.6 2.1 copy.191
  544.8 3.8 copy.192
  548.6 6.1 reshape.485
  554.7 9.2 %convert_bitcast_fusion.1 = bf16[12,256,1,384]{3,1,0,2:T(8,128)(2,1)} fusion(bf16[384,256,1]{0,1,2:T(8,128)(2,1)S(1)} %reshape.499, bf16[1,12,384,384]{3,2,1,0:T(8,128)(2,1)} %param.7, bf16[12,256,384]{2,1,0:T(8,128)(2,1)} %reshape.485, bf16[384,256]{0,1:T(8,128)(2,1)S(1)} %convert_element_type.174), kind=kOutput, calls=%fused_computation.70 | convolution fusion | flops 1850277888 | bytes 8650752 | tf_op jit(solution)/shard_map/sikc,fk->ifsc/dot_general | solution.py:100
  563.9 5.9 reshape.487
  569.8 3.3 copy.194
  573.1 57.4 %all_to_all.128 = bf16[12,128,2,1,384]{4,2,0,3,1:T(2,128)(2,1)S(1)} all-to-all(bf16[12,128,2,1,384]{4,2,0,3,1:T(2,128)(2,1)S(1)} %copy.194), channel_id=1, replica_groups=mesh['lat'=16,'batch'=2] {'lat'}, dimensions={1} | all-to-all | bytes 4718592 | tf_op jit(solution)/shard_map/all_to_all | solution.py:84
  631.2 2.4 fusion.76
  633.7 4.9 copy.198
  638.6 41.1 %all_to_all.129 = bf16[128,8,2,1,384]{4,2,1,3,0:T(2,128)(2,1)S(1)} all-to-all(bf16[128,8,2,1,384]{4,2,1,3,0:T(2,128)(2,1)} %copy.198), channel_id=1, replica_groups=mesh['lat'=16,'batch'=2] {'lat'}, dimensions={0} | all-to-all | bytes 3145728 | tf_op jit(solution)/shard_map/all_to_all | solution.py:88
  680.3 0.9 fusion.36
  681.2 0.9 fusion.34
  682.1 0.9 fusion.96
  683.0 0.9 fusion.99
  684.2 2.1 copy.201
  686.2 5.5 all-to-all-start.6
  692.0 2.1 fusion.103
  694.1 0.8 fusion.32
  694.9 0.8 fusion.102
  695.7 0.8 fusion.33
  696.6 2.7 pad_maximum_fusion
  699.3 28.5 %all-to-all-done.6 = bf16[8,128,2,1,384]{4,0,3,2,1:T(8,128)(2,1)} async-done(((bf16[8,128,2,1,384]{4,0,3,2,1:T(8,128)(2,1)}), bf16[8,128,2,1,384]{4,0,3,2,1:T(8,128)(2,1)}, u32[]{:S(2)}, u32[]{:S(2)}) %all-to-all-start.6) | async-done | bytes 1572896 | tf_op jit(solution)/shard_map/all_to_all | solution.py:92
  727.8 2.3 convert_bitcast_fusion
  730.1 3.8 copy.203
  734.0 4.9 all-to-all-start.7
  738.9 0.8 convert_element_type.173
  739.7 5.1 copy.211
  744.8 47.2 %all-to-all-done.7 = bf16[192,8,2,1,384]{4,2,1,3,0:T(2,128)(2,1)S(1)} async-done(((bf16[192,8,2,1,384]{4,2,1,3,0:T(2,128)(2,1)}), bf16[192,8,2,1,384]{4,2,1,3,0:T(2,128)(2,1)S(1)}, u32[]{:S(2)}, u32[]{:S(2)}) %all-to-all-start.7) | async-done | bytes 2359328 | tf_op jit(solution)/shard_map/all_to_all | solution.py:96
  792.5 2.4 copy.205
  794.9 2.4 reshape.492
  797.3 5.8 fusion.24
  (941 shorter events, 264.4 us)
Async XLA Ops:
  7.2 5.0 copy-start
  23.8 360.4 %all-to-all-start = ((bf16[12,128,2,1,384]{4,2,0,3,1:T(2,128)(2,1)}), bf16[12,128,2,1,384]{4,2,0,3,1:T(2,128)(2,1)}, u32[]{:S(2)}, u32[]{:S(2)}) async-start(bf16[12,128,2,1,384]{4,2,0,3,1:T(2,128)(2,1)} %copy.178), calls=%async_computation | async-start | bytes 4718592 | tf_op jit(solution)/shard_map/all_to_all | solution.py:84
  30.9 352.6 %copy-start.5 = (s32[128]{0:T(128)S(1)}, s32[128]{0:T(128)}, u32[]{:S(2)}) copy-start(s32[128]{0:T(128)} %param.9) | copy-start | bytes 1540
  386.6 48.4 %slice-start = ((s8[4718592]{0:T(1024)(128)(4,1)}), s8[524288]{0:T(1024)(128)(4,1)S(1)}, s32[]{:S(2)}) async-start(s8[4718592]{0:T(1024)(128)(4,1)} %bitcast.253), calls=%async_computation.9 | async-start | bytes 1048576
  390.9 44.1 %slice-start.1 = ((s8[4718592]{0:T(1024)(128)(4,1)}), s8[4194304]{0:T(1024)(128)(4,1)S(1)}, s32[]{:S(2)}) async-start(s8[4718592]{0:T(1024)(128)(4,1)} %bitcast.253), calls=%async_computation.10 | async-start | bytes 8388608
  484.3 58.4 %all-to-all-start.3 = ((bf16[192,8,2,1,384]{4,2,1,3,0:T(2,128)(2,1)}), bf16[192,8,2,1,384]{4,2,1,3,0:T(2,128)(2,1)}, u32[]{:S(2)}, u32[]{:S(2)}) async-start(bf16[192,8,2,1,384]{4,2,1,3,0:T(2,128)(2,1)} %copy.190), calls=%async_computation.3 | async-start | bytes 4718592 | tf_op jit(solution)/shard_map/all_to_all | solution.py:96
  631.2 49.1 %slice-start.2 = ((s8[4718592]{0:T(1024)(128)(4,1)}), s8[524288]{0:T(1024)(128)(4,1)S(1)}, s32[]{:S(2)}) async-start(s8[4718592]{0:T(1024)(128)(4,1)} %bitcast.255), calls=%async_computation.11 | async-start | bytes 1048576
  638.6 41.7 %slice-start.3 = ((s8[4718592]{0:T(1024)(128)(4,1)}), s8[4194304]{0:T(1024)(128)(4,1)S(1)}, s32[]{:S(2)}) async-start(s8[4718592]{0:T(1024)(128)(4,1)} %bitcast.255), calls=%async_computation.12 | async-start | bytes 8388608
  680.3 2.8 copy-start.2
  686.2 41.6 %all-to-all-start.6 = ((bf16[8,128,2,1,384]{4,0,3,2,1:T(8,128)(2,1)}), bf16[8,128,2,1,384]{4,0,3,2,1:T(8,128)(2,1)}, u32[]{:S(2)}, u32[]{:S(2)}) async-start(bf16[8,128,2,1,384]{4,0,3,2,1:T(8,128)(2,1)} %copy.201), calls=%async_computation.6 | async-start | bytes 3145728 | tf_op jit(solution)/shard_map/all_to_all | solution.py:92
  691.7 48.0 %all-reduce.2.cloned.1.call-start = ((), (), s32[]{:S(2)}) async-start(), calls=%async_computation.8 | async-start | bytes 9437184 | tf_op jit(solution)/shard_map/psum | solution.py:158
  692.0 2.1 copy-start.3
  734.0 4.9 copy-start.4
  734.0 58.0 %all-to-all-start.7 = ((bf16[192,8,2,1,384]{4,2,1,3,0:T(2,128)(2,1)}), bf16[192,8,2,1,384]{4,2,1,3,0:T(2,128)(2,1)S(1)}, u32[]{:S(2)}, u32[]{:S(2)}) async-start(bf16[192,8,2,1,384]{4,2,1,3,0:T(2,128)(2,1)} %copy.203), calls=%async_computation.7 | async-start | bytes 4718592 | tf_op jit(solution)/shard_map/all_to_all | solution.py:96
  797.3 5.8 copy-start.1
Sparse Core Ops, SparseCore 0:
  699.4 30.0 all-reduce.1
where the time goes:
time: 822 us; the launch traced here: 810 us
  other arithmetic  192 us (23%)
  blocking collectives  183 us (22%)
  local copies, waits for them, and re-layouts  147 us (18%)
  waiting for transfers between devices  127 us (15%)
  loops' own time  86.7 us (11%)
  matrix products  37.1 us (5%)
  starting transfers between devices  23.7 us (3%)
  between operations  15 us (2%)
    all_to_all x2, waiting for transfers between devices, to_bands(): lax.all_to_all(values, 'lat', split_axis=0, concat_axis=1, tiled=True)  98.5 us
    another operation x1, loops' own time, legendre_table(): lax.scan(advance, (zeros, zeros), jnp.arange(degree_count, dtype=jnp.int32))  86.7 us
    all_to_all x2, blocking collectives, to_degrees(): lax.all_to_all(values, 'lat', split_axis=0, concat_axis=1, tiled=True)  84.7 us
    gt x128, other arithmetic, advance(): degree > order_col + 1  82.3 us
    eq x128, other arithmetic, advance(): degree == order_col  81.4 us
    dynamic_slice x128, local copies, waits for them, and re-layouts, legendre_table(): lax.scan(advance, (zeros, zeros), jnp.arange(degree_count, dtype=jnp.int32))  79.2 us
    all_to_all x1, blocking collectives, to_orders(): lax.all_to_all(values, 'lat', split_axis=1, concat_axis=0, tiled=True)  57.4 us
    all_to_all x1, blocking collectives, back_to_orders(): lax.all_to_all(values, 'lat', split_axis=1, concat_axis=0, tiled=True)  40.7 us
  transfers between devices with their start and end apart: 5, of which 3 were waited for; matrix products, arithmetic and copies ran while one was open for 35% of the time, Pallas kernels for 0%

commit v1 on v0

--- a/solution.py
+++ b/solution.py
@@ -93,7 +93,10 @@
 
 
 def to_bands(values):
-    return lax.all_to_all(values, "lat", split_axis=0, concat_axis=1, tiled=True)
+    return jnp.concatenate(
+        lax.all_to_all(jnp.stack(jnp.split(values, lax.axis_size("lat"), axis=0)), "lat", 0, 0),
+        axis=1,
+    )
 
 
 def product(spec, left, right):

time: 822 us -> 825 us (level)
    reshape x0 -> x2, local copies, waits for them, and re-layouts: none -> 9.33 us  [to_bands(): jnp.concatenate(lax.all_to_all(jnp.stack(jnp.split(values, lax.axis_size(...]
    all_to_all x4 -> x0, local copies, waits for them, and re-layouts: 8.87 us -> none  [to_bands(): lax.all_to_all(values, 'lat', split_axis=0, concat_axis=1, tiled=True)]
    another operation x2 -> x6, local copies, waits for them, and re-layouts: 8.47 us -> 17.1 us
where the time goes in v1:
time: 825 us; the launch traced here: 814 us
  other arithmetic  192 us (23%)
  blocking collectives  183 us (22%)
  local copies, waits for them, and re-layouts  150 us (18%)
  waiting for transfers between devices  127 us (15%)
  loops' own time  86.7 us (11%)
  matrix products  37.1 us (4%)
  starting transfers between devices  23.7 us (3%)
  between operations  15.1 us (2%)
    all_to_all x2, waiting for transfers between devices, to_bands(): lax.all_to_all(jnp.stack(jnp.split(values, lax.axis_size('lat'), axis=0))...  98.5 us
    another operation x1, loops' own time, legendre_table(): lax.scan(advance, (zeros, zeros), jnp.arange(degree_count, dtype=jnp.int32))  86.7 us
    all_to_all x2, blocking collectives, to_degrees(): lax.all_to_all(values, 'lat', split_axis=0, concat_axis=1, tiled=True)  84.7 us
    gt x128, other arithmetic, advance(): degree > order_col + 1  82.3 us
    eq x128, other arithmetic, advance(): degree == order_col  81.4 us
    dynamic_slice x128, local copies, waits for them, and re-layouts, legendre_table(): lax.scan(advance, (zeros, zeros), jnp.arange(degree_count, dtype=jnp.int32))  79.2 us
    all_to_all x1, blocking collectives, to_orders(): lax.all_to_all(values, 'lat', split_axis=1, concat_axis=0, tiled=True)  57.4 us
    all_to_all x1, blocking collectives, back_to_orders(): lax.all_to_all(values, 'lat', split_axis=1, concat_axis=0, tiled=True)  40.7 us
  transfers between devices with their start and end apart: 5, of which 3 were waited for; matrix products, arithmetic and copies ran while one was open for 35% of the time, Pallas kernels for 0%

profile of v1, /device:TPU:12, one launch (start us, length us, event | category | flops | bytes accessed | tf_op | source)
XLA Modules:
  0.0 813.7 jit_solution(2072125118705137302)
XLA Ops:
  7.2 0.8 fusion.150
  8.0 0.7 fusion.105
  8.7 1.8 copy.166
  10.5 1.7 reshape.497
  12.2 3.7 convert_bitcast_fusion.3
  15.9 4.8 reshape.482
  20.8 3.0 copy.168
  23.8 7.2 all-to-all-start
  31.3 351.8 %while.21 = (s32[]{:T(128)}, f32[8,192]{1,0:T(8,128)S(1)}, f32[8,192]{1,0:T(8,128)S(1)}, f32[128,8,192]{2,1,0:T(8,128)S(1)}, s32[128]{0:T(128)S(1)}, /*index=5*/...) while((s32[]{:T(128)}, f32[8,192]{1,0:T(8,128)S(1)}, ...), condition=%wide.region_2.3_spmd.clone.clone.clone.clone, body=%wide.region_1.2_spmd.clone.clone.clone.clone.sunk | while | flops 18991 | bytes 48339 | solution.py:50
  51.8 0.6 compare_bitcast_fusion.5
  54.6 0.6 compare_bitcast_fusion.5
  57.3 0.6 compare_bitcast_fusion.5
  60.1 0.6 compare_bitcast_fusion.5
  62.8 0.6 compare_bitcast_fusion.5
  65.6 0.6 compare_bitcast_fusion.5
  68.3 0.6 compare_bitcast_fusion.5
  71.1 0.6 compare_bitcast_fusion.5
  73.8 0.6 compare_bitcast_fusion.5
  76.6 0.6 compare_bitcast_fusion.5
  384.1 2.1 copy.237
  386.6 1.4 fusion.79
  388.0 2.9 copy.173
  390.9 43.5 %all_to_all.106 = bf16[128,8,2,1,384]{4,2,1,3,0:T(2,128)(2,1)S(1)} all-to-all(bf16[128,8,2,1,384]{4,2,1,3,0:T(2,128)(2,1)} %copy.173), channel_id=1, replica_groups=mesh['lat'=16,'batch'=2] {'lat'}, dimensions={0} | all-to-all | bytes 3145728 | tf_op jit(solution)/shard_map/all_to_all | solution.py:88
  435.1 0.7 fusion.40
  435.7 0.7 fusion.38
  436.4 0.7 fusion.90
  437.1 0.7 fusion.93
  438.0 0.9 copy.178
  439.0 40.7 %all_to_all.107 = bf16[8,128,2,1,384]{4,0,3,2,1:T(8,128)(2,1)S(1)} all-to-all(bf16[8,128,2,1,384]{4,0,3,2,1:T(8,128)(2,1)S(1)} %copy.178), channel_id=1, replica_groups=mesh['lat'=16,'batch'=2] {'lat'}, dimensions={1} | all-to-all | bytes 3145728 | tf_op jit(solution)/shard_map/all_to_all | solution.py:92
  479.7 0.8 convert_bitcast_fusion.2
  481.4 2.4 copy.180
  483.8 5.8 all-to-all-start.3
  489.7 0.8 multiply_convert_fusion.1
  490.9 51.3 %all-to-all-done.3 = bf16[16,12,8,2,1,384]{5,2,4,3,1,0:T(8,128)(2,1)} async-done(((bf16[16,12,8,2,1,384]{5,2,4,3,1,0:T(8,128)(2,1)}), bf16[16,12,8,2,1,384]{5,2,4,3,1,0:T(8,128)(2,1)}, u32[]{:S(2)}, u32[]{:S(2)}) %all-to-all-start.3) | async-done | bytes 2359328 | tf_op jit(solution)/shard_map/all_to_all | solution.py:97
  542.2 5.5 copy.181
  547.7 6.1 reshape.488
  553.8 9.2 %convert_bitcast_fusion.1 = bf16[12,256,1,384]{3,1,0,2:T(8,128)(2,1)} fusion(bf16[384,256,1]{0,1,2:T(8,128)(2,1)S(1)} %reshape.503, bf16[1,12,384,384]{3,2,1,0:T(8,128)(2,1)} %param.7, bf16[12,256,384]{2,1,0:T(8,128)(2,1)} %reshape.488, bf16[384,256]{0,1:T(8,128)(2,1)S(1)} %convert_element_type.174), kind=kOutput, calls=%fused_computation.70 | convolution fusion | flops 1850277888 | bytes 8650752 | tf_op jit(solution)/shard_map/sikc,fk->ifsc/dot_general | solution.py:103
  562.9 5.9 reshape.490
  568.9 3.3 copy.183
  572.2 57.4 %all_to_all.108 = bf16[12,128,2,1,384]{4,2,0,3,1:T(2,128)(2,1)S(1)} all-to-all(bf16[12,128,2,1,384]{4,2,0,3,1:T(2,128)(2,1)S(1)} %copy.183), channel_id=1, replica_groups=mesh['lat'=16,'batch'=2] {'lat'}, dimensions={1} | all-to-all | bytes 4718592 | tf_op jit(solution)/shard_map/all_to_all | solution.py:84
  630.3 2.4 fusion.76
  632.7 4.9 copy.187
  637.6 41.1 %all_to_all.109 = bf16[128,8,2,1,384]{4,2,1,3,0:T(2,128)(2,1)S(1)} all-to-all(bf16[128,8,2,1,384]{4,2,1,3,0:T(2,128)(2,1)} %copy.187), channel_id=1, replica_groups=mesh['lat'=16,'batch'=2] {'lat'}, dimensions={0} | all-to-all | bytes 3145728 | tf_op jit(solution)/shard_map/all_to_all | solution.py:88
  679.4 0.9 fusion.36
  680.3 0.9 fusion.34
  681.2 0.9 fusion.96
  682.1 0.9 fusion.99
  683.2 2.1 copy.190
  685.3 5.5 all-to-all-start.6
  691.1 2.1 fusion.103
  693.2 0.8 fusion.32
  694.0 0.8 fusion.102
  694.8 0.8 fusion.33
  695.6 2.7 pad_maximum_fusion
  698.4 28.5 %all-to-all-done.6 = bf16[8,128,2,1,384]{4,0,3,2,1:T(8,128)(2,1)} async-done(((bf16[8,128,2,1,384]{4,0,3,2,1:T(8,128)(2,1)}), bf16[8,128,2,1,384]{4,0,3,2,1:T(8,128)(2,1)}, u32[]{:S(2)}, u32[]{:S(2)}) %all-to-all-start.6) | async-done | bytes 1572896 | tf_op jit(solution)/shard_map/all_to_all | solution.py:92
  726.9 2.3 convert_bitcast_fusion
  730.2 2.4 copy.192
  732.6 4.9 all-to-all-start.7
  737.5 0.8 convert_element_type.173
  738.3 5.1 copy.199
  743.4 47.2 %all-to-all-done.7 = bf16[16,12,8,2,1,384]{5,2,4,3,1,0:T(8,128)(2,1)S(1)} async-done(((bf16[16,12,8,2,1,384]{5,2,4,3,1,0:T(8,128)(2,1)}), bf16[16,12,8,2,1,384]{5,2,4,3,1,0:T(8,128)(2,1)S(1)}, u32[]{:S(2)}, u32[]{:S(2)}) %all-to-all-start.7) | async-done | bytes 2359328 | tf_op jit(solution)/shard_map/all_to_all | solution.py:97
  790.6 3.8 copy.193
  794.5 6.1 reshape.496
  800.6 5.8 fusion.24
  (971 shorter events, 265.1 us)
Async XLA Ops:
  7.2 5.0 copy-start
  23.8 360.4 %all-to-all-start = ((bf16[12,128,2,1,384]{4,2,0,3,1:T(2,128)(2,1)}), bf16[12,128,2,1,384]{4,2,0,3,1:T(2,128)(2,1)}, u32[]{:S(2)}, u32[]{:S(2)}) async-start(bf16[12,128,2,1,384]{4,2,0,3,1:T(2,128)(2,1)} %copy.168), calls=%async_computation | async-start | bytes 4718592 | tf_op jit(solution)/shard_map/all_to_all | solution.py:84
  30.9 352.6 %copy-start.5 = (s32[128]{0:T(128)S(1)}, s32[128]{0:T(128)}, u32[]{:S(2)}) copy-start(s32[128]{0:T(128)} %param.9) | copy-start | bytes 1540
  386.6 48.4 %slice-start = ((s8[4718592]{0:T(1024)(128)(4,1)}), s8[524288]{0:T(1024)(128)(4,1)S(1)}, s32[]{:S(2)}) async-start(s8[4718592]{0:T(1024)(128)(4,1)} %bitcast.377), calls=%async_computation.9 | async-start | bytes 1048576
  390.9 44.1 %slice-start.1 = ((s8[4718592]{0:T(1024)(128)(4,1)}), s8[4194304]{0:T(1024)(128)(4,1)S(1)}, s32[]{:S(2)}) async-start(s8[4718592]{0:T(1024)(128)(4,1)} %bitcast.377), calls=%async_computation.10 | async-start | bytes 8388608
  483.8 58.4 %all-to-all-start.3 = ((bf16[16,12,8,2,1,384]{5,2,4,3,1,0:T(8,128)(2,1)}), bf16[16,12,8,2,1,384]{5,2,4,3,1,0:T(8,128)(2,1)}, u32[]{:S(2)}, u32[]{:S(2)}) async-start(bf16[16,12,8,2,1,384]{5,2,4,3,1,0:T(8,128)(2,1)} %copy.180), calls=%async_computation.3 | async-start | bytes 4718592 | tf_op jit(solution)/shard_map/all_to_all | solution.py:97
  630.3 49.1 %slice-start.2 = ((s8[4718592]{0:T(1024)(128)(4,1)}), s8[524288]{0:T(1024)(128)(4,1)S(1)}, s32[]{:S(2)}) async-start(s8[4718592]{0:T(1024)(128)(4,1)} %bitcast.379), calls=%async_computation.11 | async-start | bytes 1048576
  637.6 41.7 %slice-start.3 = ((s8[4718592]{0:T(1024)(128)(4,1)}), s8[4194304]{0:T(1024)(128)(4,1)S(1)}, s32[]{:S(2)}) async-start(s8[4718592]{0:T(1024)(128)(4,1)} %bitcast.379), calls=%async_computation.12 | async-start | bytes 8388608
  679.3 2.8 copy-start.2
  685.3 41.6 %all-to-all-start.6 = ((bf16[8,128,2,1,384]{4,0,3,2,1:T(8,128)(2,1)}), bf16[8,128,2,1,384]{4,0,3,2,1:T(8,128)(2,1)}, u32[]{:S(2)}, u32[]{:S(2)}) async-start(bf16[8,128,2,1,384]{4,0,3,2,1:T(8,128)(2,1)} %copy.190), calls=%async_computation.6 | async-start | bytes 3145728 | tf_op jit(solution)/shard_map/all_to_all | solution.py:92
  690.8 47.5 %all-reduce.2.cloned.1.call-start = ((), (), s32[]{:S(2)}) async-start(), calls=%async_computation.8 | async-start | bytes 9437184 | tf_op jit(solution)/shard_map/psum | solution.py:161
  691.1 2.1 copy-start.3
  732.6 4.9 copy-start.4
  732.6 58.0 %all-to-all-start.7 = ((bf16[16,12,8,2,1,384]{5,2,4,3,1,0:T(8,128)(2,1)}), bf16[16,12,8,2,1,384]{5,2,4,3,1,0:T(8,128)(2,1)S(1)}, u32[]{:S(2)}, u32[]{:S(2)}) async-start(bf16[16,12,8,2,1,384]{5,2,4,3,1,0:T(8,128)(2,1)} %copy.192), calls=%async_computation.7 | async-start | bytes 4718592 | tf_op jit(solution)/shard_map/all_to_all | solution.py:97
  800.6 5.8 copy-start.1
Sparse Core Ops, SparseCore 0:
  698.5 30.0 all-reduce.1
